TPU v7x, 32 devices: a whole 2x2x4 slice. The times are simulated.
32 devices in a mesh: section: 4 (over y, core), replica: 8 (over z, x).
Axes of the slice: x: 2, y: 2, z: 4, core: 2. Of those that a mesh axis runs over, the one named last changes fastest.
Arguments:
- gradient: bfloat16 [512, 32768], P('section', 'replica'), may hold values from -1300 to 1300
- residual: float32 [512, 32768], P('section', 'replica'), may hold values from -6 to 6
- block_ids: int32 [4, 64], P('section', 'replica'), may hold values from 0 to 15, as said below
- block_counts: int32 [4, 8], P('section', 'replica'), may hold values from 1 to 8, as said below
Outputs:
- new_residual: float32 [512, 32768], P('section', 'replica')
- update: bfloat16 [512, 4096], P('section', 'replica')
Inputs may be any that keep to these rules, and one draw needn't show every extreme that they name: `block_ids`: each device's 8 block numbers are distinct; only the first block_counts of them are selected. `block_counts`: in every section some replica selects exactly 8 blocks; the others select at most 4.
All inputs are finite; a program needn't handle non-finite values.
Results may differ from a plain program's by a relative error of at most 0.013.
Values may be sent and summed in bfloat16 or wider, within the bound.
A program may use at most 64 MiB of HBM per device.

v0:
```python
import functools

import jax
import jax.numpy as jnp
from jax import lax
from jax.experimental import pallas as pl
from jax.experimental.pallas import tpu as pltpu
from jax.sharding import PartitionSpec as P

BLK = 8
CHUNKS = 4
LANES = 128
MESH = pl.DeviceIdType.MESH

scale_level = 1.0
epsilon = 1e-06


def kernel(
    sections,
    replicas,
    ids_hbm,
    counts_hbm,
    gradient_ref,
    residual_ref,
    update_ref,
    left_ref,
    grad_buf,
    acc_buf,
    packed,
    received,
    target_row,
    targets,
    square_row,
    squares,
    load_sems,
    ids_ref,
    counts_ref,
    list_sems,
    relayed,
    far_targets,
    far_data,
    cross_buf,
    cross_in,
    relay_sems,
    near_row_sems,
    near_sems,
    far_row_sems,
    far_sems,
    cross_sems,
    norm_send,
    norm_recv,
):
    row_count, width = gradient_ref.shape
    block_total = row_count // BLK
    slot_count = ids_hbm.shape[1]
    slot_rows = slot_count * BLK
    cap = slot_count // 2
    cap_rows = cap * BLK
    half = replicas // 2
    col_count = width // replicas
    section = lax.axis_index("section")
    replica = lax.axis_index("replica")
    total = sections * replicas

    def ahead(here, extent):
        return [here] + [
            jnp.where(here + k >= extent, here + k - extent, here + k) for k in range(1, extent)
        ]

    section_at = ahead(section, sections)
    replica_at = ahead(replica, replicas)
    others = [(i, j) for i in range(sections) for j in range(replicas) if i + j > 0]

    lists = [
        pltpu.make_async_copy(ids_hbm, ids_ref, list_sems.at[0]),
        pltpu.make_async_copy(counts_hbm, counts_ref, list_sems.at[1]),
    ]
    for copy in lists:
        copy.start()

    step = row_count // CHUNKS
    loads = []
    for c in range(CHUNKS):
        rows = pl.ds(c * step, step)
        blocks = pl.ds(c * step // BLK, step // BLK)
        one = pltpu.make_async_copy(gradient_ref.at[rows], grad_buf.at[rows], load_sems.at[0, c])
        two = pltpu.make_async_copy(residual_ref.at[blocks], acc_buf.at[blocks], load_sems.at[1, c])
        one.start()
        two.start()
        loads.append((one, two))

    barrier = pltpu.get_barrier_semaphore()

    for i, j in others:
        pl.semaphore_signal(
            barrier,
            inc=1,
            device_id={"section": section_at[i], "replica": replica_at[j]},
            device_id_type=MESH,
        )

    for copy in lists:
        copy.wait()
    lane = lax.broadcasted_iota(jnp.int32, (1, LANES), 1)
    row = jnp.full((1, LANES), -1, jnp.int32)
    for s in range(slot_count):
        base = jnp.where(s < counts_ref[0, 0], ids_ref[0, s] * BLK, -2 * row_count)
        row = jnp.where(lane // BLK == s, base + lane % BLK, row)
    target_row[...] = row

    for c in range(CHUNKS):
        for copy in loads[c]:
            copy.wait()
        rows = pl.ds(c * step, step)
        blocks = pl.ds(c * step // BLK, step // BLK)
        value = grad_buf[rows].astype(jnp.float32).reshape(step // BLK, BLK, width)
        acc_buf[blocks] = acc_buf[blocks] + value

    for s in range(0, slot_count, 2):
        pair = [acc_buf[ids_ref[0, s + i]] for i in range(2)]
        if s >= cap:
            pair = [jnp.where(s + i < counts_ref[0, 0], pair[i], 0.0) for i in range(2)]
        pair = jnp.concatenate(pair, axis=0).astype(jnp.bfloat16)
        for p in range(replicas):
            packed[p, pl.ds(s * BLK, 2 * BLK), :] = pair[:, p * col_count : (p + 1) * col_count]

    pl.semaphore_wait(barrier, total - 1)

    side = replica // half * half
    other_side = half - side
    place_in_side = replica - side
    inner = [
        jnp.where(place_in_side + k >= half, place_in_side + k - half, place_in_side + k)
        for k in range(half)
    ]

    def send(src, dst, sems, slot, peer):
        copy = pltpu.make_async_remote_copy(
            src_ref=src,
            dst_ref=dst,
            send_sem=sems.at[0, slot],
            recv_sem=sems.at[1, slot],
            device_id={"replica": peer},
            device_id_type=MESH,
        )
        copy.start()
        return copy

    relay_in, near_rows, near, far_rows, far = {}, {}, {}, {}, {}
    for k in range(half - 1, 0, -1):
        peer = side + inner[k]
        source = packed.at[other_side + inner[k], pl.ds(cap_rows, slot_rows - cap_rows)]
        relay_in[k] = send(source, relayed.at[k - 1], relay_sems, k - 1, peer)
    for k in range(half - 1, -1, -1):
        peer = other_side + inner[k]
        far_rows[k] = send(target_row, far_targets.at[k], far_row_sems, k, peer)
        far[k] = send(packed.at[peer, pl.ds(0, cap_rows)], far_data.at[k], far_sems, k, peer)
    for k in range(half - 1, 0, -1):
        peer = side + inner[k]
        near_rows[k] = send(target_row, targets.at[k - 1], near_row_sems, k - 1, peer)
        near[k] = send(packed.at[peer], received.at[k - 1], near_sems, k - 1, peer)

    for c in range(CHUNKS):
        for b in range(c * step // BLK, (c + 1) * step // BLK):
            chosen = jnp.int32(0)
            for s in range(slot_count):
                hit = (ids_ref[0, s] == b) & (s < counts_ref[0, 0])
                chosen = jnp.where(hit, 1, chosen)
            value = acc_buf[b]
            rounded = value.astype(jnp.bfloat16).astype(jnp.float32)
            left_ref[b] = value - jnp.where(chosen > 0, rounded, 0.0)


    def place(wanted, block):
        row_iota = lax.broadcasted_iota(jnp.int32, (row_count, wanted.shape[1]), 0)
        hot = jnp.where(row_iota == wanted, 1.0, 0.0).astype(jnp.bfloat16)
        return jnp.dot(hot, block, preferred_element_type=jnp.float32)

    crossing = packed[other_side + place_in_side, cap_rows:, :].astype(jnp.float32)
    for k in range(1, half):
        relay_in[k].wait_recv()
        crossing = crossing + relayed[k - 1].astype(jnp.float32)
    cross_buf[...] = crossing.astype(jnp.bfloat16)
    cross = send(cross_buf, cross_in, cross_sems, 0, other_side + place_in_side)

    summed = place(target_row[:, :slot_rows], packed[replica])
    for k in range(1, half):
        near_rows[k].wait_recv()
        near[k].wait_recv()
        summed = summed + place(targets[k - 1][:, :slot_rows], received[k - 1])
    wanted = jnp.full((1, slot_rows), -1, jnp.int32)
    for k in range(half):
        far_rows[k].wait_recv()
        far[k].wait_recv()
        theirs = far_targets[k][:, :slot_rows]
        wanted = jnp.maximum(wanted, theirs)
        summed = summed + place(theirs[:, :cap_rows], far_data[k])
    cross.wait_recv()
    summed = summed + place(wanted[:, cap_rows:], cross_in[...])

    lanes = jnp.sum(summed * summed, axis=0, keepdims=True)
    part = lanes[:, :LANES]
    for j in range(1, col_count // LANES):
        part = part + lanes[:, j * LANES : (j + 1) * LANES]
    square_row[...] = part

    for slot, (i, j) in enumerate(others):
        pltpu.make_async_remote_copy(
            src_ref=square_row,
            dst_ref=squares.at[slot],
            send_sem=norm_send,
            recv_sem=norm_recv,
            device_id={"section": section_at[i], "replica": replica_at[j]},
            device_id_type=MESH,
        ).start()
    for group in (relay_in, near_rows, near, far_rows, far, {0: cross}):
        for copy in group.values():
            copy.wait_send()
    pltpu.make_async_copy(squares, squares, norm_recv).wait()
    pltpu.make_async_copy(squares, squares, norm_send).wait()
    norm_total = jnp.sum(part + jnp.sum(squares[...], axis=0), axis=1, keepdims=True)
    element_count = sections * row_count * width
    root_mean = jnp.sqrt(norm_total / element_count + epsilon)
    clip_factor = scale_level / root_mean
    update_ref[...] = (summed * clip_factor).astype(jnp.bfloat16)


def per_device(sections, replicas, gradient, residual, block_ids, block_counts):
    row_count, width = gradient.shape
    block_total = row_count // BLK
    slot_count = block_ids.shape[1]
    col_count = width // replicas
    total = sections * replicas
    slot_rows = slot_count * BLK
    over_rows = slot_rows - slot_count // 2 * BLK
    half = replicas // 2
    update, left = pl.pallas_call(
        functools.partial(kernel, sections, replicas),
        out_shape=(
            pltpu.VMEM((row_count, col_count), jnp.bfloat16),
            pltpu.VMEM((block_total, BLK, width), jnp.float32),
        ),
        in_specs=[
            pl.BlockSpec(memory_space=pl.ANY),
            pl.BlockSpec(memory_space=pl.ANY),
            pl.BlockSpec(memory_space=pl.ANY),
            pl.BlockSpec(memory_space=pl.ANY),
        ],
        out_specs=(
            pl.BlockSpec(memory_space=pltpu.VMEM),
            pl.BlockSpec(memory_space=pltpu.VMEM),
        ),
        scratch_shapes=[
            pltpu.VMEM((row_count, width), jnp.bfloat16),
            pltpu.VMEM((block_total, BLK, width), jnp.float32),
            pltpu.VMEM((replicas, slot_rows, col_count), jnp.bfloat16),
            pltpu.VMEM((half - 1, slot_rows, col_count), jnp.bfloat16),
            pltpu.VMEM((1, LANES), jnp.int32),
            pltpu.VMEM((half - 1, 1, LANES), jnp.int32),
            pltpu.VMEM((1, LANES), jnp.float32),
            pltpu.VMEM((total - 1, 1, LANES), jnp.float32),
            pltpu.SemaphoreType.DMA((2, CHUNKS)),
            pltpu.SMEM(block_ids.shape, jnp.int32),
            pltpu.SMEM(block_counts.shape, jnp.int32),
            pltpu.SemaphoreType.DMA((2,)),
            pltpu.VMEM((half - 1, over_rows, col_count), jnp.bfloat16),
            pltpu.VMEM((half, 1, LANES), jnp.int32),
            pltpu.VMEM((half, slot_rows - over_rows, col_count), jnp.bfloat16),
            pltpu.VMEM((over_rows, col_count), jnp.bfloat16),
            pltpu.VMEM((over_rows, col_count), jnp.bfloat16),
            pltpu.SemaphoreType.DMA((2, half - 1)),
            pltpu.SemaphoreType.DMA((2, half - 1)),
            pltpu.SemaphoreType.DMA((2, half - 1)),
            pltpu.SemaphoreType.DMA((2, half)),
            pltpu.SemaphoreType.DMA((2, half)),
            pltpu.SemaphoreType.DMA((2, 1)),
            pltpu.SemaphoreType.DMA,
            pltpu.SemaphoreType.DMA,
        ],
        compiler_params=pltpu.CompilerParams(collective_id=0, has_side_effects=True),
    )(block_ids, block_counts, gradient, residual.reshape(block_total, BLK, width))

    return (left.reshape(row_count, width), update)


def solution(mesh):
    spec = P("section", "replica")
    sizes = (mesh.shape["section"], mesh.shape["replica"])
    return jax.shard_map(
        functools.partial(per_device, *sizes),
        mesh=mesh,
        in_specs=(spec,) * 4,
        out_specs=(spec, spec),
        check_vma=False,
    )
```

profile of v0, /device:TPU:0, one launch (start us, length us, event | category | flops | bytes accessed | tf_op | source)
XLA Modules:
  0.0 24.6 jit_solution(15493856532713030258)
XLA Ops:
  1.3 21.4 %shard_map.59 = (bf16[128,512]{1,0:T(8,128)(2,1)S(1)}, f32[16,8,4096]{2,1,0:T(8,128)S(1)}) custom-call(s32[1,8]{1,0:T(1,128)} %ids_hbm.1, s32[1,1]{1,0:T(1,128)S(6)} %copy.10.counts_hbm, bf16[128,4096]{1,0:T(8,128)(2,1)} %gradient_ref.1, f32[16,8,4096]{2,1,0:T(8,128)} %bitcast.3), custom_call_target="tpu_custom_call" | custom-call | tf_op jit(solution)/shard_map/pallas_call | solution.py:238
  22.6 1.3 %copy.8 = f32[128,4096]{1,0:T(8,128)} copy(f32[128,4096]{1,0:T(8,128)S(1)} %bitcast.2) | data formatting | bytes 4194304
  24.0 0.7 %copy.9 = bf16[128,512]{1,0:T(8,128)(2,1)} copy(bf16[128,512]{1,0:T(8,128)(2,1)S(1)} %get-tuple-element.7) | data formatting | bytes 262144
where the time goes:
time: 24.8 us; the launch traced here: 24.6 us
  Pallas kernels  21.4 us (86%)
  local copies, waits for them, and re-layouts  1.98 us (8%)
  between operations  1.29 us (5%)
    pallas_call x1, Pallas kernels, per_device(): pl.pallas_call(functools.partial(kernel, sections, replicas), out_shape=(...  21.4 us
    unnamed x2, local copies, waits for them, and re-layouts  1.98 us

commit v1 on v0

--- a/solution.py
+++ b/solution.py
@@ -92,7 +92,8 @@
 
     barrier = pltpu.get_barrier_semaphore()
 
-    for i, j in others:
+    greeted = [(i, j) for i, j in others if i == 0 or j == 0]
+    for i, j in greeted:
         pl.semaphore_signal(
             barrier,
             inc=1,
@@ -125,7 +126,7 @@
         for p in range(replicas):
             packed[p, pl.ds(s * BLK, 2 * BLK), :] = pair[:, p * col_count : (p + 1) * col_count]
 
-    pl.semaphore_wait(barrier, total - 1)
+    pl.semaphore_wait(barrier, len(greeted))
 
     side = replica // half * half
     other_side = half - side
@@ -226,6 +227,18 @@
     update_ref[...] = (summed * clip_factor).astype(jnp.bfloat16)
 
 
+def finish(update_ref, left_ref, update_out, left_out, sems):
+    copies = [pltpu.make_async_copy(update_ref, update_out, sems.at[0])]
+    parts = left_ref.shape[0] // CHUNKS
+    for c in range(CHUNKS):
+        part = pl.ds(c * parts, parts)
+        copies.append(pltpu.make_async_copy(left_ref.at[part], left_out.at[part], sems.at[c + 1]))
+    for copy in copies:
+        copy.start()
+    for copy in copies:
+        copy.wait()
+
+
 def per_device(sections, replicas, gradient, residual, block_ids, block_counts):
     row_count, width = gradient.shape
     block_total = row_count // BLK
@@ -242,10 +255,10 @@
             pltpu.VMEM((block_total, BLK, width), jnp.float32),
         ),
         in_specs=[
-            pl.BlockSpec(memory_space=pl.ANY),
-            pl.BlockSpec(memory_space=pl.ANY),
-            pl.BlockSpec(memory_space=pl.ANY),
-            pl.BlockSpec(memory_space=pl.ANY),
+            pl.BlockSpec(memory_space=pltpu.HBM),
+            pl.BlockSpec(memory_space=pltpu.HBM),
+            pl.BlockSpec(memory_space=pltpu.HBM),
+            pl.BlockSpec(memory_space=pltpu.HBM),
         ],
         out_specs=(
             pl.BlockSpec(memory_space=pltpu.VMEM),
@@ -281,6 +294,17 @@
         compiler_params=pltpu.CompilerParams(collective_id=0, has_side_effects=True),
     )(block_ids, block_counts, gradient, residual.reshape(block_total, BLK, width))
 
+    update, left = pl.pallas_call(
+        finish,
+        out_shape=(
+            jax.ShapeDtypeStruct(update.shape, update.dtype),
+            jax.ShapeDtypeStruct(left.shape, left.dtype),
+        ),
+        in_specs=[pl.BlockSpec(memory_space=pltpu.VMEM)] * 2,
+        out_specs=(pl.BlockSpec(memory_space=pltpu.HBM),) * 2,
+        scratch_shapes=[pltpu.SemaphoreType.DMA((CHUNKS + 1,))],
+        compiler_params=pltpu.CompilerParams(vmem_limit_bytes=1 << 20),
+    )(update, left)
     return (left.reshape(row_count, width), update)
 
 

time: 24.8 us -> 23.5 us (0.948)
  local copies, waits for them, and re-layouts: 1.98 us -> 0 us
  Pallas kernels: 21.4 us -> 22.1 us
    unnamed x2 -> x0, local copies, waits for them, and re-layouts: 1.98 us -> none
    pallas_call x0 -> x1, Pallas kernels: none -> 1.4 us  [per_device(): pl.pallas_call(finish, out_shape=(jax.ShapeDtypeStruct(update.shape, upda...]
    pallas_call x1, Pallas kernels: 21.4 us -> 20.7 us  [per_device(): pl.pallas_call(functools.partial(kernel, sections, replicas), out_shape=(...]
where the time goes in v1:
time: 23.5 us; the launch traced here: 23.4 us
  Pallas kernels  22.1 us (94%)
  between operations  1.29 us (5%)
    pallas_call x1, Pallas kernels, per_device(): pl.pallas_call(functools.partial(kernel, sections, replicas), out_shape=(...  20.7 us
    pallas_call x1, Pallas kernels, per_device(): pl.pallas_call(finish, out_shape=(jax.ShapeDtypeStruct(update.shape, upda...  1.4 us

profile of v1, /device:TPU:0, one launch (start us, length us, event | category | flops | bytes accessed | tf_op | source)
XLA Modules:
  0.0 23.4 jit_solution(1793610192652326374)
XLA Ops:
  1.3 20.7 %shard_map.59 = (bf16[128,512]{1,0:T(8,128)(2,1)S(1)}, f32[16,8,4096]{2,1,0:T(8,128)S(1)}) custom-call(s32[1,8]{1,0:T(1,128)} %ids_hbm.1, s32[1,1]{1,0:T(1,128)S(6)} %copy.6.counts_hbm, bf16[128,4096]{1,0:T(8,128)(2,1)} %gradient_ref.1, f32[16,8,4096]{2,1,0:T(8,128)} %bitcast.2), custom_call_target="tpu_custom_call" | custom-call | tf_op jit(solution)/shard_map/pallas_call | solution.py:251
  22.0 1.4 %shard_map.60 = (bf16[128,512]{1,0:T(8,128)(2,1)}, f32[16,8,4096]{2,1,0:T(8,128)}) custom-call(bf16[128,512]{1,0:T(8,128)(2,1)S(1)} %get-tuple-element.6.update_ref, f32[16,8,4096]{2,1,0:T(8,128)S(1)} %get-tuple-element.7.left_ref), custom_call_target="tpu_custom_call" | custom-call | tf_op jit(solution)/shard_map/pallas_call | solution.py:297

commit v2 on v0

v2 whole, which is shorter than its diff:
```python
import functools

import jax
import jax.numpy as jnp
from jax import lax
from jax.experimental import pallas as pl
from jax.experimental.pallas import tpu as pltpu
from jax.sharding import PartitionSpec as P

BLK = 8
LANES = 128
EARLY_STEPS = 8
MESH = pl.DeviceIdType.MESH

scale_level = 1.0
epsilon = 1e-06


def flip(index, mask):
    bit, out = 1, index
    while bit <= mask:
        if mask & bit:
            out = out + bit - 2 * bit * (index // bit % 2)
        bit *= 2
    return out


def exchange(
    sections,
    replicas,
    ids_hbm,
    counts_hbm,
    gradient_hbm,
    residual_hbm,
    early_hbm,
    update_ref,
    left_ref,
    grad_buf,
    res_buf,
    packed,
    target_row,
    ids_ref,
    counts_ref,
    list_sems,
    load_sems,
    ready,
    relayed,
    near_rows_buf,
    near_buf,
    far_rows_buf,
    far_buf,
    cross_buf,
    cross_in,
    relay_sems,
    near_row_sems,
    near_sems,
    far_row_sems,
    far_sems,
    cross_sems,
    square_row,
    squares,
    norm_send,
    norm_recv,
):
    block_total, _, width = residual_hbm.shape
    row_count = block_total * BLK
    slot_count = ids_hbm.shape[1]
    slot_rows = slot_count * BLK
    cap = slot_count // 2
    cap_rows = cap * BLK
    half = replicas // 2
    col_count = width // replicas
    section = lax.axis_index("section")
    replica = lax.axis_index("replica")

    def ahead(here, extent):
        return [here] + [
            jnp.where(here + k >= extent, here + k - extent, here + k) for k in range(1, extent)
        ]

    section_at = ahead(section, sections)
    peer_at = [flip(replica, mask) for mask in range(replicas)]
    others = [(i, j) for i in range(sections) for j in range(replicas) if i + j > 0]

    quarter = replicas // 4
    part_at = replica // quarter
    lower = part_at < 2
    inner = (part_at == 1) | (part_at == 2)
    beside = [half + quarter + low for low in range(quarter)]
    beyond = [half + low for low in range(quarter)]

    def greet(i, j):
        pl.semaphore_signal(
            barrier,
            inc=1,
            device_id={"section": section_at[i], "replica": peer_at[j]},
            device_id_type=MESH,
        )

    barrier = pltpu.get_barrier_semaphore()
    for j in range(1, half):
        greet(0, j)
    for i in range(1, sections):
        greet(i, 0)
    for j in beside:
        pl.when(lower | inner)(functools.partial(greet, 0, j))
    for j in beyond:
        pl.when(lower | (part_at == 3))(functools.partial(greet, 0, j))
    greeted = half - 1 + sections - 1 + jnp.where(part_at == 0, 0, half)

    lists = [
        pltpu.make_async_copy(ids_hbm, ids_ref, list_sems.at[0]),
        pltpu.make_async_copy(counts_hbm, counts_ref, list_sems.at[1]),
    ]
    for copy in lists:
        copy.start()

    order = list(range(replicas - 1, -1, -1))
    same = list(range(1, quarter))
    next_to = list(range(quarter, half))
    loads = {}
    for mask in order:
        cols = pl.ds(pl.multiple_of(peer_at[mask] * col_count, col_count), col_count)
        loads[mask] = (
            pltpu.make_async_copy(gradient_hbm.at[:, :, cols], grad_buf[mask], load_sems.at[0, mask]),
            pltpu.make_async_copy(residual_hbm.at[:, :, cols], res_buf[mask], load_sems.at[1, mask]),
        )
        for copy in loads[mask]:
            copy.start()

    for copy in lists:
        copy.wait()
    count = counts_ref[0, 0]
    ids = [ids_ref[0, s] for s in range(slot_count)]
    lane = lax.broadcasted_iota(jnp.int32, (1, LANES), 1)
    row = jnp.full((1, LANES), -1, jnp.int32)
    for s in range(slot_count):
        base = jnp.where(s < count, ids[s] * BLK, -2 * row_count)
        row = jnp.where(lane // BLK == s, base + lane % BLK, row)
    target_row[...] = row

    def pack(mask):
        for copy in loads[mask]:
            copy.wait()
        for s in range(0, slot_count, 2):
            pair = []
            for i in (s, s + 1):
                value = grad_buf[mask][ids[i]].astype(jnp.float32) + res_buf[mask][ids[i]]
                if s >= cap:
                    value = jnp.where(i < count, value, 0.0)
                pair.append(value)
            packed[mask, pl.ds(s * BLK, 2 * BLK), :] = jnp.concatenate(pair, axis=0).astype(jnp.bfloat16)

    def make(src, dst, sems, slot, peer):
        return pltpu.make_async_remote_copy(
            src_ref=src,
            dst_ref=dst,
            send_sem=sems.at[0, slot],
            recv_sem=sems.at[1, slot],
            device_id={"replica": peer},
            device_id_type=MESH,
        )

    relay_in, near_rows, near, far_rows, far = {}, {}, {}, {}, {}
    for mask in range(1, half):
        peer = peer_at[mask]
        relay_in[mask] = make(
            packed.at[half + mask, pl.ds(cap_rows, slot_rows - cap_rows)],
            relayed.at[mask - 1],
            relay_sems,
            mask - 1,
            peer,
        )
        near_rows[mask] = make(target_row, near_rows_buf.at[mask - 1], near_row_sems, mask - 1, peer)
        near[mask] = make(packed.at[mask], near_buf.at[mask - 1], near_sems, mask - 1, peer)
    for mask in range(half, replicas):
        peer, slot = peer_at[mask], mask - half
        far_rows[mask] = make(target_row, far_rows_buf.at[slot], far_row_sems, slot, peer)
        far[mask] = make(packed.at[mask, pl.ds(0, cap_rows)], far_buf.at[slot], far_sems, slot, peer)
    cross = make(cross_buf, cross_in, cross_sems, 0, peer_at[half])

    def start_far(masks):
        for mask in masks:
            far_rows[mask].start()
            far[mask].start()

    def tell(mask):
        pl.semaphore_signal(ready, inc=1, device_id={"replica": peer_at[mask]}, device_id_type=MESH)

    def start_near(masks):
        for mask in masks[::-1]:
            near_rows[mask].start()
            near[mask].start()

    for mask in order[: half - 1]:
        pack(mask)
    pl.semaphore_wait(barrier, greeted)
    pl.when(part_at == 1)(functools.partial(tell, quarter))
    for mask in range(half - 1, 0, -1):
        relay_in[mask].start()
    pl.when(inner)(functools.partial(start_far, beside))
    pack(half)
    pl.when(inner)(functools.partial(start_far, beyond))
    for mask in order[half:]:
        pack(mask)
    for mask in range(half - 1, 0, -1):
        relay_in[mask].wait_send()

    @pl.when(part_at == 3)
    def _():
        start_far(beside)
        start_far(beyond)

    start_near(next_to)
    start_near(same)

    @pl.when(part_at == 0)
    def _():
        pl.semaphore_wait(ready, 1)
        start_far(beside)
        start_far(beyond)

    for b in range(block_total):
        chosen = jnp.int32(0)
        for s in range(slot_count):
            chosen = jnp.where((ids[s] == b) & (s < count), 1, chosen)
        for mask in order:
            value = grad_buf[mask][b].astype(jnp.float32) + res_buf[mask][b]
            rounded = value.astype(jnp.bfloat16).astype(jnp.float32)
            left_ref[mask, b] = value - jnp.where(chosen > 0, rounded, 0.0)

    def place(wanted, block):
        row_iota = lax.broadcasted_iota(jnp.int32, (row_count, wanted.shape[1]), 0)
        hot = jnp.where(row_iota == wanted, 1.0, 0.0).astype(jnp.bfloat16)
        return jnp.dot(hot, block, preferred_element_type=jnp.float32)

    crossing = packed[half, cap_rows:, :].astype(jnp.float32)
    for mask in range(half - 1, 0, -1):
        relay_in[mask].wait_recv()
        crossing = crossing + relayed[mask - 1].astype(jnp.float32)
    cross_buf[...] = crossing.astype(jnp.bfloat16)
    cross.start()

    summed = place(target_row[:, :slot_rows], packed[0])
    for mask in range(half - 1, 0, -1):
        near_rows[mask].wait_recv()
        near[mask].wait_recv()
        summed = summed + place(near_rows_buf[mask - 1][:, :slot_rows], near_buf[mask - 1])
    wanted = jnp.full((1, slot_rows), -1, jnp.int32)
    for mask in range(replicas - 1, half - 1, -1):
        far_rows[mask].wait_recv()
        far[mask].wait_recv()
        theirs = far_rows_buf[mask - half][:, :slot_rows]
        wanted = jnp.maximum(wanted, theirs)
        summed = summed + place(theirs[:, :cap_rows], far_buf[mask - half])
    cross.wait_recv()
    summed = summed + place(wanted[:, cap_rows:], cross_in[...])

    lanes = jnp.sum(summed * summed, axis=0, keepdims=True)
    part = lanes[:, :LANES]
    for j in range(1, col_count // LANES):
        part = part + lanes[:, j * LANES : (j + 1) * LANES]
    square_row[...] = part

    for slot, (i, j) in reversed(list(enumerate(others))):
        pltpu.make_async_remote_copy(
            src_ref=square_row,
            dst_ref=squares.at[slot],
            send_sem=norm_send,
            recv_sem=norm_recv,
            device_id={"section": section_at[i], "replica": peer_at[j]},
            device_id_type=MESH,
        ).start()
    for group in (near_rows, near, far_rows, far, {0: cross}):
        for copy in group.values():
            copy.wait_send()
    pltpu.make_async_copy(squares, squares, norm_recv).wait()
    pltpu.make_async_copy(squares, squares, norm_send).wait()
    norm_total = jnp.sum(part + jnp.sum(squares[...], axis=0), axis=1, keepdims=True)
    element_count = sections * row_count * width
    root_mean = jnp.sqrt(norm_total / element_count + epsilon)
    clip_factor = scale_level / root_mean
    update_ref[...] = (summed * clip_factor).astype(jnp.bfloat16)


def residual_early(early, ids_hbm, counts_hbm, gradient_hbm, residual_hbm, left_hbm, *scratch):
    grad_buf, res_buf, ids_ref, counts_ref, list_sems, load_sems, out_sems = scratch
    block_total = residual_hbm.shape[0]
    slot_count = ids_hbm.shape[1]
    step = block_total // EARLY_STEPS

    @pl.when(early())
    def _():
        lists = [
            pltpu.make_async_copy(ids_hbm, ids_ref, list_sems.at[0]),
            pltpu.make_async_copy(counts_hbm, counts_ref, list_sems.at[1]),
        ]
        for copy in lists:
            copy.start()
        loads, stores = [], []
        for c in range(EARLY_STEPS):
            part = pl.ds(c * step, step)
            loads.append(
                (
                    pltpu.make_async_copy(gradient_hbm.at[part], grad_buf.at[part], load_sems.at[0, c]),
                    pltpu.make_async_copy(residual_hbm.at[part], res_buf.at[part], load_sems.at[1, c]),
                )
            )
            stores.append(pltpu.make_async_copy(res_buf.at[part], left_hbm.at[part], out_sems.at[c]))
            for copy in loads[c]:
                copy.start()
        for copy in lists:
            copy.wait()
        for c in range(EARLY_STEPS):
            for copy in loads[c]:
                copy.wait()
            for b in range(c * step, (c + 1) * step):
                chosen = jnp.int32(0)
                for s in range(slot_count):
                    chosen = jnp.where((ids_ref[0, s] == b) & (s < counts_ref[0, 0]), 1, chosen)
                value = grad_buf[b].astype(jnp.float32) + res_buf[b]
                rounded = value.astype(jnp.bfloat16).astype(jnp.float32)
                res_buf[b] = value - jnp.where(chosen > 0, rounded, 0.0)
            stores[c].start()
        for copy in stores:
            copy.wait()


def starts_early():
    return (lax.axis_index("replica") == 0) & (lax.axis_index("section") < 2)


def deliver(replicas, early, update_ref, left_ref, early_hbm, update_hbm, left_hbm, sems):
    col_count = left_ref.shape[3]
    replica = lax.axis_index("replica")
    update_copy = pltpu.make_async_copy(update_ref, update_hbm, sems.at[replicas])
    update_copy.start()

    @pl.when(jnp.logical_not(early()))
    def _():
        copies = []
        for mask in range(replicas):
            cols = pl.ds(pl.multiple_of(flip(replica, mask) * col_count, col_count), col_count)
            copies.append(pltpu.make_async_copy(left_ref.at[mask], left_hbm.at[:, :, cols], sems.at[mask]))
        for copy in copies:
            copy.start()
        for copy in copies:
            copy.wait()

    update_copy.wait()


def per_device(sections, replicas, gradient, residual, block_ids, block_counts):
    row_count, width = gradient.shape
    block_total = row_count // BLK
    slot_count = block_ids.shape[1]
    col_count = width // replicas
    total = sections * replicas
    slot_rows = slot_count * BLK
    cap_rows = slot_count // 2 * BLK
    over_rows = slot_rows - cap_rows
    half = replicas // 2
    pair = pltpu.SemaphoreType.DMA
    gradient = gradient.reshape(block_total, BLK, width)
    residual = residual.reshape(block_total, BLK, width)
    early = pl.pallas_call(
        functools.partial(residual_early, starts_early),
        out_shape=jax.ShapeDtypeStruct(residual.shape, residual.dtype),
        in_specs=[pl.BlockSpec(memory_space=pl.ANY)] * 4,
        out_specs=pl.BlockSpec(memory_space=pltpu.HBM),
        scratch_shapes=[
            pltpu.VMEM(gradient.shape, gradient.dtype),
            pltpu.VMEM(residual.shape, residual.dtype),
            pltpu.SMEM(block_ids.shape, jnp.int32),
            pltpu.SMEM(block_counts.shape, jnp.int32),
            pair((2,)),
            pair((2, EARLY_STEPS)),
            pair((EARLY_STEPS,)),
        ],
    )(block_ids, block_counts, gradient, residual)
    update, left = pl.pallas_call(
        functools.partial(exchange, sections, replicas),
        out_shape=(
            pltpu.VMEM((row_count, col_count), jnp.bfloat16),
            pltpu.VMEM((replicas, block_total, BLK, col_count), jnp.float32),
        ),
        in_specs=[pl.BlockSpec(memory_space=pl.ANY)] * 5,
        out_specs=(pl.BlockSpec(memory_space=pltpu.VMEM),) * 2,
        scratch_shapes=[
            [pltpu.VMEM((block_total, BLK, col_count), jnp.bfloat16)] * replicas,
            [pltpu.VMEM((block_total, BLK, col_count), jnp.float32)] * replicas,
            pltpu.VMEM((replicas, slot_rows, col_count), jnp.bfloat16),
            pltpu.VMEM((1, LANES), jnp.int32),
            pltpu.SMEM(block_ids.shape, jnp.int32),
            pltpu.SMEM(block_counts.shape, jnp.int32),
            pair((2,)),
            pair((2, replicas)),
            pltpu.SemaphoreType.REGULAR,
            pltpu.VMEM((half - 1, over_rows, col_count), jnp.bfloat16),
            pltpu.VMEM((half - 1, 1, LANES), jnp.int32),
            pltpu.VMEM((half - 1, slot_rows, col_count), jnp.bfloat16),
            pltpu.VMEM((half, 1, LANES), jnp.int32),
            pltpu.VMEM((half, cap_rows, col_count), jnp.bfloat16),
            pltpu.VMEM((over_rows, col_count), jnp.bfloat16),
            pltpu.VMEM((over_rows, col_count), jnp.bfloat16),
            pair((2, half - 1)),
            pair((2, half - 1)),
            pair((2, half - 1)),
            pair((2, half)),
            pair((2, half)),
            pair((2, 1)),
            pltpu.VMEM((1, LANES), jnp.float32),
            pltpu.VMEM((total - 1, 1, LANES), jnp.float32),
            pltpu.SemaphoreType.DMA,
            pltpu.SemaphoreType.DMA,
        ],
        compiler_params=pltpu.CompilerParams(collective_id=0, has_side_effects=True),
    )(
        block_ids,
        block_counts,
        gradient,
        residual,
        early,
    )
    update, left = pl.pallas_call(
        functools.partial(deliver, replicas, starts_early),
        out_shape=(
            jax.ShapeDtypeStruct(update.shape, update.dtype),
            jax.ShapeDtypeStruct((block_total, BLK, width), left.dtype),
        ),
        in_specs=[pl.BlockSpec(memory_space=pl.ANY)] * 2 + [pl.BlockSpec(memory_space=pltpu.HBM)],
        out_specs=(pl.BlockSpec(memory_space=pltpu.HBM),) * 2,
        input_output_aliases={2: 1},
        scratch_shapes=[pltpu.SemaphoreType.DMA((replicas + 1,))],
        compiler_params=pltpu.CompilerParams(vmem_limit_bytes=1 << 20),
    )(update, left, early)
    return (left.reshape(row_count, width), update)


def solution(mesh):
    spec = P("section", "replica")
    sizes = (mesh.shape["section"], mesh.shape["replica"])
    return jax.shard_map(
        functools.partial(per_device, *sizes),
        mesh=mesh,
        in_specs=(spec,) * 4,
        out_specs=(spec, spec),
        check_vma=False,
    )
```

time: 24.8 us -> 22.8 us (0.919)
  local copies, waits for them, and re-layouts: 1.98 us -> 0 us
    unnamed x2 -> x0, local copies, waits for them, and re-layouts: 1.98 us -> none
    pallas_call x1 -> x3, Pallas kernels: 21.4 us -> 21.3 us  [the longest x1 17.7 us: per_device(): pl.pallas_call(functools.partial(exchange, sections, replicas), out_shape...]
where the time goes in v2:
time: 22.8 us; the launch traced here: 22.6 us
  Pallas kernels  21.3 us (93%)
  between operations  1.29 us (6%)
    pallas_call x1, Pallas kernels, per_device(): pl.pallas_call(functools.partial(exchange, sections, replicas), out_shape...  17.7 us
    pallas_call x1, Pallas kernels, per_device(): pl.pallas_call(functools.partial(residual_early, starts_early), out_shape...  2.87 us
    pallas_call x1, Pallas kernels, per_device(): pl.pallas_call(functools.partial(deliver, replicas, starts_early), out_sh...  0.74 us

profile of v2, /device:TPU:0, one launch (start us, length us, event | category | flops | bytes accessed | tf_op | source)
XLA Modules:
  0.0 22.6 jit_solution(16802347851477919422)
XLA Ops:
  1.3 2.9 %shard_map.59.early_hbm = f32[16,8,4096]{2,1,0:T(8,128)} custom-call(s32[1,8]{1,0:T(1,128)} %ids_hbm.3, s32[1,1]{1,0:T(1,128)S(6)} %copy.8.counts_hbm, bf16[16,8,4096]{2,1,0:T(8,128)(2,1)} %bitcast.6, f32[16,8,4096]{2,1,0:T(8,128)} %bitcast.4), custom_call_target="tpu_custom_call" | custom-call | tf_op jit(solution)/shard_map/pallas_call | solution.py:366
  4.2 17.7 %shard_map.60 = (bf16[128,512]{1,0:T(8,128)(2,1)S(1)}, f32[8,16,8,512]{3,2,1,0:T(8,128)S(1)}) custom-call(s32[1,8]{1,0:T(1,128)} %ids_hbm.3, s32[1,1]{1,0:T(1,128)S(6)} %copy.8.counts_hbm, bf16[16,8,4096]{2,1,0:T(8,128)(2,1)} %bitcast.7, f32[16,8,4096]{2,1,0:T(8,128)} %bitcast.5, f32[16,8,4096]{2,1,0:T(8,128)} %shard_map.59.early_hbm), custom_call_target="tpu_custom_call" | custom-call | tf_op jit(solution)/shard_map/pallas_call | solution.py:381
  21.9 0.7 %shard_map.61 = (bf16[128,512]{1,0:T(8,128)(2,1)}, f32[16,8,4096]{2,1,0:T(8,128)}) custom-call(bf16[128,512]{1,0:T(8,128)(2,1)S(1)} %get-tuple-element.6.update_ref, f32[8,16,8,512]{3,2,1,0:T(8,128)S(1)} %get-tuple-element.7.left_ref, f32[16,8,4096]{2,1,0:T(8,128)} %shard_map.59.early_hbm), custom_call_target="tpu_custom_call", output_to_operand_aliasing={{1}: (2, {})} | custom-call | tf_op jit(solution)/shard_map/pallas_call | solution.py:425

commit v3 on v2

--- a/solution.py
+++ b/solution.py
@@ -57,6 +57,11 @@
     far_row_sems,
     far_sems,
     cross_sems,
+    mate_buf,
+    over_buf,
+    near_over,
+    mate_sems,
+    over_sems,
     square_row,
     squares,
     norm_send,
@@ -172,11 +177,22 @@
             peer,
         )
         near_rows[mask] = make(target_row, near_rows_buf.at[mask - 1], near_row_sems, mask - 1, peer)
-        near[mask] = make(packed.at[mask], near_buf.at[mask - 1], near_sems, mask - 1, peer)
+        rows = pl.ds(0, slot_rows if mask in same else cap_rows)
+        near[mask] = make(packed.at[mask, rows], near_buf.at[mask - 1, rows], near_sems, mask - 1, peer)
     for mask in range(half, replicas):
         peer, slot = peer_at[mask], mask - half
         far_rows[mask] = make(target_row, far_rows_buf.at[slot], far_row_sems, slot, peer)
         far[mask] = make(packed.at[mask, pl.ds(0, cap_rows)], far_buf.at[slot], far_sems, slot, peer)
+    mate = {}
+    for mask in same:
+        mate[mask] = make(
+            packed.at[quarter + mask, pl.ds(cap_rows, slot_rows - cap_rows)],
+            mate_buf.at[mask - 1],
+            mate_sems,
+            mask - 1,
+            peer_at[mask],
+        )
+    over = make(over_buf, near_over, over_sems, 0, peer_at[quarter])
     cross = make(cross_buf, cross_in, cross_sems, 0, peer_at[half])
 
     def start_far(masks):
@@ -188,37 +204,40 @@
         pl.semaphore_signal(ready, inc=1, device_id={"replica": peer_at[mask]}, device_id_type=MESH)
 
     def start_near(masks):
-        for mask in masks[::-1]:
+        for mask in masks:
             near_rows[mask].start()
             near[mask].start()
 
-    for mask in order[: half - 1]:
+    urgent = order[: half - 1]
+    for mask in urgent:
         pack(mask)
     pl.semaphore_wait(barrier, greeted)
     pl.when(part_at == 1)(functools.partial(tell, quarter))
-    for mask in range(half - 1, 0, -1):
+    for mask in next_to[::-1] + same:
         relay_in[mask].start()
     pl.when(inner)(functools.partial(start_far, beside))
     pack(half)
-    pl.when(inner)(functools.partial(start_far, beyond))
+    pl.when(inner)(functools.partial(start_far, beyond[::-1]))
     for mask in order[half:]:
-        pack(mask)
+        if mask not in urgent:
+            pack(mask)
+    for mask in same:
+        mate[mask].start()
+    @pl.when(part_at == 3)
+    def _():
+        start_far(beyond[::-1])
+        start_far(beside)
+
     for mask in range(half - 1, 0, -1):
         relay_in[mask].wait_send()
-
-    @pl.when(part_at == 3)
-    def _():
-        start_far(beside)
-        start_far(beyond)
-
-    start_near(next_to)
-    start_near(same)
 
     @pl.when(part_at == 0)
     def _():
         pl.semaphore_wait(ready, 1)
         start_far(beside)
-        start_far(beyond)
+        start_far(beyond[::-1])
+
+    start_near(next_to[::-1] + same)
 
     for b in range(block_total):
         chosen = jnp.int32(0)
@@ -240,12 +259,26 @@
         crossing = crossing + relayed[mask - 1].astype(jnp.float32)
     cross_buf[...] = crossing.astype(jnp.bfloat16)
     cross.start()
+    beside_over = packed[quarter, cap_rows:, :].astype(jnp.float32)
+    for mask in same:
+        mate[mask].wait_recv()
+        beside_over = beside_over + mate_buf[mask - 1].astype(jnp.float32)
+    over_buf[...] = beside_over.astype(jnp.bfloat16)
+    over.start()
 
     summed = place(target_row[:, :slot_rows], packed[0])
+    wanted = jnp.full((1, slot_rows), -1, jnp.int32)
     for mask in range(half - 1, 0, -1):
         near_rows[mask].wait_recv()
         near[mask].wait_recv()
-        summed = summed + place(near_rows_buf[mask - 1][:, :slot_rows], near_buf[mask - 1])
+        theirs = near_rows_buf[mask - 1][:, :slot_rows]
+        if mask in same:
+            summed = summed + place(theirs, near_buf[mask - 1])
+        else:
+            wanted = jnp.maximum(wanted, theirs)
+            summed = summed + place(theirs[:, :cap_rows], near_buf[mask - 1, :cap_rows])
+    over.wait_recv()
+    summed = summed + place(wanted[:, cap_rows:], near_over[...])
     wanted = jnp.full((1, slot_rows), -1, jnp.int32)
     for mask in range(replicas - 1, half - 1, -1):
         far_rows[mask].wait_recv()
@@ -271,7 +304,7 @@
             device_id={"section": section_at[i], "replica": peer_at[j]},
             device_id_type=MESH,
         ).start()
-    for group in (near_rows, near, far_rows, far, {0: cross}):
+    for group in (near_rows, near, far_rows, far, mate, {0: cross, 1: over}):
         for copy in group.values():
             copy.wait_send()
     pltpu.make_async_copy(squares, squares, norm_recv).wait()
@@ -409,6 +442,11 @@
             pair((2, half)),
             pair((2, half)),
             pair((2, 1)),
+            pltpu.VMEM((half // 2 - 1, over_rows, col_count), jnp.bfloat16),
+            pltpu.VMEM((over_rows, col_count), jnp.bfloat16),
+            pltpu.VMEM((over_rows, col_count), jnp.bfloat16),
+            pair((2, half // 2 - 1)),
+            pair((2, 1)),
             pltpu.VMEM((1, LANES), jnp.float32),
             pltpu.VMEM((total - 1, 1, LANES), jnp.float32),
             pltpu.SemaphoreType.DMA,

time: 22.8 us -> 22.5 us (0.987)
  Pallas kernels: 21.3 us -> 21 us
    pallas_call x1, Pallas kernels: 17.7 us -> 17.4 us  [per_device(): pl.pallas_call(functools.partial(exchange, sections, replicas), out_shape...]
where the time goes in v3:
time: 22.5 us; the launch traced here: 22.3 us
  Pallas kernels  21 us (93%)
  between operations  1.29 us (6%)
    pallas_call x1, Pallas kernels, per_device(): pl.pallas_call(functools.partial(exchange, sections, replicas), out_shape...  17.4 us
    pallas_call x1, Pallas kernels, per_device(): pl.pallas_call(functools.partial(residual_early, starts_early), out_shape...  2.87 us
    pallas_call x1, Pallas kernels, per_device(): pl.pallas_call(functools.partial(deliver, replicas, starts_early), out_sh...  0.74 us

profile of v3, /device:TPU:0, one launch (start us, length us, event | category | flops | bytes accessed | tf_op | source)
XLA Modules:
  0.0 22.3 jit_solution(14633177202658376745)
XLA Ops:
  1.3 2.9 %shard_map.59.early_hbm = f32[16,8,4096]{2,1,0:T(8,128)} custom-call(s32[1,8]{1,0:T(1,128)} %ids_hbm.3, s32[1,1]{1,0:T(1,128)S(6)} %copy.8.counts_hbm, bf16[16,8,4096]{2,1,0:T(8,128)(2,1)} %bitcast.6, f32[16,8,4096]{2,1,0:T(8,128)} %bitcast.4), custom_call_target="tpu_custom_call" | custom-call | tf_op jit(solution)/shard_map/pallas_call | solution.py:399
  4.2 17.4 %shard_map.60 = (bf16[128,512]{1,0:T(8,128)(2,1)S(1)}, f32[8,16,8,512]{3,2,1,0:T(8,128)S(1)}) custom-call(s32[1,8]{1,0:T(1,128)} %ids_hbm.3, s32[1,1]{1,0:T(1,128)S(6)} %copy.8.counts_hbm, bf16[16,8,4096]{2,1,0:T(8,128)(2,1)} %bitcast.7, f32[16,8,4096]{2,1,0:T(8,128)} %bitcast.5, f32[16,8,4096]{2,1,0:T(8,128)} %shard_map.59.early_hbm), custom_call_target="tpu_custom_call" | custom-call | tf_op jit(solution)/shard_map/pallas_call | solution.py:414
  21.6 0.7 %shard_map.61 = (bf16[128,512]{1,0:T(8,128)(2,1)}, f32[16,8,4096]{2,1,0:T(8,128)}) custom-call(bf16[128,512]{1,0:T(8,128)(2,1)S(1)} %get-tuple-element.6.update_ref, f32[8,16,8,512]{3,2,1,0:T(8,128)S(1)} %get-tuple-element.7.left_ref, f32[16,8,4096]{2,1,0:T(8,128)} %shard_map.59.early_hbm), custom_call_target="tpu_custom_call", output_to_operand_aliasing={{1}: (2, {})} | custom-call | tf_op jit(solution)/shard_map/pallas_call | solution.py:463

commit v4 on v3

--- a/solution.py
+++ b/solution.py
@@ -87,6 +87,13 @@
     peer_at = [flip(replica, mask) for mask in range(replicas)]
     others = [(i, j) for i in range(sections) for j in range(replicas) if i + j > 0]
 
+    lists = [
+        pltpu.make_async_copy(ids_hbm, ids_ref, list_sems.at[0]),
+        pltpu.make_async_copy(counts_hbm, counts_ref, list_sems.at[1]),
+    ]
+    for copy in lists:
+        copy.start()
+
     quarter = replicas // 4
     part_at = replica // quarter
     lower = part_at < 2
@@ -110,15 +117,8 @@
     for j in beside:
         pl.when(lower | inner)(functools.partial(greet, 0, j))
     for j in beyond:
-        pl.when(lower | (part_at == 3))(functools.partial(greet, 0, j))
-    greeted = half - 1 + sections - 1 + jnp.where(part_at == 0, 0, half)
-
-    lists = [
-        pltpu.make_async_copy(ids_hbm, ids_ref, list_sems.at[0]),
-        pltpu.make_async_copy(counts_hbm, counts_ref, list_sems.at[1]),
-    ]
-    for copy in lists:
-        copy.start()
+        pl.when(lower)(functools.partial(greet, 0, j))
+    greeted = half - 1 + sections - 1 + jnp.where(lower, jnp.where(inner, quarter, 0), half)
 
     order = list(range(replicas - 1, -1, -1))
     same = list(range(1, quarter))
@@ -144,10 +144,12 @@
         row = jnp.where(lane // BLK == s, base + lane % BLK, row)
     target_row[...] = row
 
-    def pack(mask):
+    def arrive(mask):
         for copy in loads[mask]:
             copy.wait()
-        for s in range(0, slot_count, 2):
+
+    def pack_slots(mask, first, last):
+        for s in range(first, last, 2):
             pair = []
             for i in (s, s + 1):
                 value = grad_buf[mask][ids[i]].astype(jnp.float32) + res_buf[mask][ids[i]]
@@ -155,6 +157,10 @@
                     value = jnp.where(i < count, value, 0.0)
                 pair.append(value)
             packed[mask, pl.ds(s * BLK, 2 * BLK), :] = jnp.concatenate(pair, axis=0).astype(jnp.bfloat16)
+
+    def pack(mask):
+        arrive(mask)
+        pack_slots(mask, 0, slot_count)
 
     def make(src, dst, sems, slot, peer):
         return pltpu.make_async_remote_copy(
@@ -210,14 +216,21 @@
 
     urgent = order[: half - 1]
     for mask in urgent:
-        pack(mask)
+        arrive(mask)
+        pack_slots(mask, cap, slot_count)
     pl.semaphore_wait(barrier, greeted)
-    pl.when(part_at == 1)(functools.partial(tell, quarter))
-    for mask in next_to[::-1] + same:
+    @pl.when(part_at == 2)
+    def _():
+        tell(half + quarter)
+        tell(half)
+
+    for mask in next_to + same:
         relay_in[mask].start()
+    for mask in urgent:
+        pack_slots(mask, 0, cap)
     pl.when(inner)(functools.partial(start_far, beside))
     pack(half)
-    pl.when(inner)(functools.partial(start_far, beyond[::-1]))
+    pl.when(part_at == 2)(functools.partial(start_far, beyond[::-1]))
     for mask in order[half:]:
         if mask not in urgent:
             pack(mask)
@@ -227,6 +240,11 @@
     def _():
         start_far(beyond[::-1])
         start_far(beside)
+
+    @pl.when(part_at == 1)
+    def _():
+        pl.semaphore_wait(ready, 1)
+        start_far(beyond[::-1])
 
     for mask in range(half - 1, 0, -1):
         relay_in[mask].wait_send()

time: 22.5 us -> 22.2 us (0.987)
    pallas_call x1, Pallas kernels: 17.4 us -> 17.2 us  [per_device(): pl.pallas_call(functools.partial(exchange, sections, replicas), out_shape...]
where the time goes in v4:
time: 22.2 us; the launch traced here: 22.1 us
  Pallas kernels  20.8 us (94%)
  between operations  1.29 us (6%)
    pallas_call x1, Pallas kernels, per_device(): pl.pallas_call(functools.partial(exchange, sections, replicas), out_shape...  17.2 us
    pallas_call x1, Pallas kernels, per_device(): pl.pallas_call(functools.partial(residual_early, starts_early), out_shape...  2.87 us
    pallas_call x1, Pallas kernels, per_device(): pl.pallas_call(functools.partial(deliver, replicas, starts_early), out_sh...  0.74 us

profile of v4, /device:TPU:0, one launch (start us, length us, event | category | flops | bytes accessed | tf_op | source)
XLA Modules:
  0.0 22.1 jit_solution(17669249138392583756)
XLA Ops:
  1.3 2.9 %shard_map.59.early_hbm = f32[16,8,4096]{2,1,0:T(8,128)} custom-call(s32[1,8]{1,0:T(1,128)} %ids_hbm.3, s32[1,1]{1,0:T(1,128)S(6)} %copy.8.counts_hbm, bf16[16,8,4096]{2,1,0:T(8,128)(2,1)} %bitcast.6, f32[16,8,4096]{2,1,0:T(8,128)} %bitcast.4), custom_call_target="tpu_custom_call" | custom-call | tf_op jit(solution)/shard_map/pallas_call | solution.py:417
  4.2 17.2 %shard_map.60 = (bf16[128,512]{1,0:T(8,128)(2,1)S(1)}, f32[8,16,8,512]{3,2,1,0:T(8,128)S(1)}) custom-call(s32[1,8]{1,0:T(1,128)} %ids_hbm.3, s32[1,1]{1,0:T(1,128)S(6)} %copy.8.counts_hbm, bf16[16,8,4096]{2,1,0:T(8,128)(2,1)} %bitcast.7, f32[16,8,4096]{2,1,0:T(8,128)} %bitcast.5, f32[16,8,4096]{2,1,0:T(8,128)} %shard_map.59.early_hbm), custom_call_target="tpu_custom_call" | custom-call | tf_op jit(solution)/shard_map/pallas_call | solution.py:432
  21.3 0.7 %shard_map.61 = (bf16[128,512]{1,0:T(8,128)(2,1)}, f32[16,8,4096]{2,1,0:T(8,128)}) custom-call(bf16[128,512]{1,0:T(8,128)(2,1)S(1)} %get-tuple-element.6.update_ref, f32[8,16,8,512]{3,2,1,0:T(8,128)S(1)} %get-tuple-element.7.left_ref, f32[16,8,4096]{2,1,0:T(8,128)} %shard_map.59.early_hbm), custom_call_target="tpu_custom_call", output_to_operand_aliasing={{1}: (2, {})} | custom-call | tf_op jit(solution)/shard_map/pallas_call | solution.py:481

commit v5 on v4

--- a/solution.py
+++ b/solution.py
@@ -224,7 +224,7 @@
         tell(half + quarter)
         tell(half)
 
-    for mask in next_to + same:
+    for mask in next_to[::-1] + same:
         relay_in[mask].start()
     for mask in urgent:
         pack_slots(mask, 0, cap)
@@ -295,17 +295,17 @@
         else:
             wanted = jnp.maximum(wanted, theirs)
             summed = summed + place(theirs[:, :cap_rows], near_buf[mask - 1, :cap_rows])
-    over.wait_recv()
-    summed = summed + place(wanted[:, cap_rows:], near_over[...])
-    wanted = jnp.full((1, slot_rows), -1, jnp.int32)
+    far_wanted = jnp.full((1, slot_rows), -1, jnp.int32)
     for mask in range(replicas - 1, half - 1, -1):
         far_rows[mask].wait_recv()
         far[mask].wait_recv()
         theirs = far_rows_buf[mask - half][:, :slot_rows]
-        wanted = jnp.maximum(wanted, theirs)
+        far_wanted = jnp.maximum(far_wanted, theirs)
         summed = summed + place(theirs[:, :cap_rows], far_buf[mask - half])
+    over.wait_recv()
+    summed = summed + place(wanted[:, cap_rows:], near_over[...])
     cross.wait_recv()
-    summed = summed + place(wanted[:, cap_rows:], cross_in[...])
+    summed = summed + place(far_wanted[:, cap_rows:], cross_in[...])
 
     lanes = jnp.sum(summed * summed, axis=0, keepdims=True)
     part = lanes[:, :LANES]
@@ -313,7 +313,12 @@
         part = part + lanes[:, j * LANES : (j + 1) * LANES]
     square_row[...] = part
 
-    for slot, (i, j) in reversed(list(enumerate(others))):
+    far_first = sorted(
+        enumerate(others),
+        key=lambda entry: (entry[1][0] * 2 // sections, entry[1][0] % 2 == 0, entry[1][1]),
+        reverse=True,
+    )
+    for slot, (i, j) in far_first:
         pltpu.make_async_remote_copy(
             src_ref=square_row,
             dst_ref=squares.at[slot],

time: 22.2 us -> 22 us (level)
  no operation moved by 1% of the time
where the time goes in v5:
time: 22 us; the launch traced here: 21.8 us
  Pallas kernels  20.6 us (94%)
  between operations  1.29 us (6%)
    pallas_call x1, Pallas kernels, per_device(): pl.pallas_call(functools.partial(exchange, sections, replicas), out_shape...  16.9 us
    pallas_call x1, Pallas kernels, per_device(): pl.pallas_call(functools.partial(residual_early, starts_early), out_shape...  2.87 us
    pallas_call x1, Pallas kernels, per_device(): pl.pallas_call(functools.partial(deliver, replicas, starts_early), out_sh...  0.74 us

profile of v5, /device:TPU:0, one launch (start us, length us, event | category | flops | bytes accessed | tf_op | source)
XLA Modules:
  0.0 21.8 jit_solution(14875732927733635269)
XLA Ops:
  1.3 2.9 %shard_map.59.early_hbm = f32[16,8,4096]{2,1,0:T(8,128)} custom-call(s32[1,8]{1,0:T(1,128)} %ids_hbm.3, s32[1,1]{1,0:T(1,128)S(6)} %copy.8.counts_hbm, bf16[16,8,4096]{2,1,0:T(8,128)(2,1)} %bitcast.6, f32[16,8,4096]{2,1,0:T(8,128)} %bitcast.4), custom_call_target="tpu_custom_call" | custom-call | tf_op jit(solution)/shard_map/pallas_call | solution.py:422
  4.2 16.9 %shard_map.60 = (bf16[128,512]{1,0:T(8,128)(2,1)S(1)}, f32[8,16,8,512]{3,2,1,0:T(8,128)S(1)}) custom-call(s32[1,8]{1,0:T(1,128)} %ids_hbm.3, s32[1,1]{1,0:T(1,128)S(6)} %copy.8.counts_hbm, bf16[16,8,4096]{2,1,0:T(8,128)(2,1)} %bitcast.7, f32[16,8,4096]{2,1,0:T(8,128)} %bitcast.5, f32[16,8,4096]{2,1,0:T(8,128)} %shard_map.59.early_hbm), custom_call_target="tpu_custom_call" | custom-call | tf_op jit(solution)/shard_map/pallas_call | solution.py:437
  21.1 0.7 %shard_map.61 = (bf16[128,512]{1,0:T(8,128)(2,1)}, f32[16,8,4096]{2,1,0:T(8,128)}) custom-call(bf16[128,512]{1,0:T(8,128)(2,1)S(1)} %get-tuple-element.6.update_ref, f32[8,16,8,512]{3,2,1,0:T(8,128)S(1)} %get-tuple-element.7.left_ref, f32[16,8,4096]{2,1,0:T(8,128)} %shard_map.59.early_hbm), custom_call_target="tpu_custom_call", output_to_operand_aliasing={{1}: (2, {})} | custom-call | tf_op jit(solution)/shard_map/pallas_call | solution.py:486

commit v6 on v5

--- a/solution.py
+++ b/solution.py
@@ -9,7 +9,7 @@
 
 BLK = 8
 LANES = 128
-EARLY_STEPS = 8
+EARLY_STEPS = 2
 MESH = pl.DeviceIdType.MESH
 
 scale_level = 1.0
@@ -45,16 +45,14 @@
     load_sems,
     ready,
     relayed,
-    near_rows_buf,
+    rows_buf,
     near_buf,
-    far_rows_buf,
     far_buf,
     cross_buf,
     cross_in,
     relay_sems,
-    near_row_sems,
+    row_sems,
     near_sems,
-    far_row_sems,
     far_sems,
     cross_sems,
     mate_buf,
@@ -182,12 +180,12 @@
             mask - 1,
             peer,
         )
-        near_rows[mask] = make(target_row, near_rows_buf.at[mask - 1], near_row_sems, mask - 1, peer)
+        near_rows[mask] = make(target_row, rows_buf.at[mask - 1], row_sems, 0, peer)
         rows = pl.ds(0, slot_rows if mask in same else cap_rows)
         near[mask] = make(packed.at[mask, rows], near_buf.at[mask - 1, rows], near_sems, mask - 1, peer)
     for mask in range(half, replicas):
         peer, slot = peer_at[mask], mask - half
-        far_rows[mask] = make(target_row, far_rows_buf.at[slot], far_row_sems, slot, peer)
+        far_rows[mask] = make(target_row, rows_buf.at[mask - 1], row_sems, 0, peer)
         far[mask] = make(packed.at[mask, pl.ds(0, cap_rows)], far_buf.at[slot], far_sems, slot, peer)
     mate = {}
     for mask in same:
@@ -285,11 +283,11 @@
     over.start()
 
     summed = place(target_row[:, :slot_rows], packed[0])
+    pltpu.make_async_copy(rows_buf, rows_buf, row_sems.at[1, 0]).wait()
     wanted = jnp.full((1, slot_rows), -1, jnp.int32)
     for mask in range(half - 1, 0, -1):
-        near_rows[mask].wait_recv()
         near[mask].wait_recv()
-        theirs = near_rows_buf[mask - 1][:, :slot_rows]
+        theirs = rows_buf[mask - 1][:, :slot_rows]
         if mask in same:
             summed = summed + place(theirs, near_buf[mask - 1])
         else:
@@ -297,9 +295,8 @@
             summed = summed + place(theirs[:, :cap_rows], near_buf[mask - 1, :cap_rows])
     far_wanted = jnp.full((1, slot_rows), -1, jnp.int32)
     for mask in range(replicas - 1, half - 1, -1):
-        far_rows[mask].wait_recv()
         far[mask].wait_recv()
-        theirs = far_rows_buf[mask - half][:, :slot_rows]
+        theirs = rows_buf[mask - 1][:, :slot_rows]
         far_wanted = jnp.maximum(far_wanted, theirs)
         summed = summed + place(theirs[:, :cap_rows], far_buf[mask - half])
     over.wait_recv()
@@ -327,7 +324,8 @@
             device_id={"section": section_at[i], "replica": peer_at[j]},
             device_id_type=MESH,
         ).start()
-    for group in (near_rows, near, far_rows, far, mate, {0: cross, 1: over}):
+    pltpu.make_async_copy(rows_buf, rows_buf, row_sems.at[0, 0]).wait()
+    for group in (near, far, mate, {0: cross, 1: over}):
         for copy in group.values():
             copy.wait_send()
     pltpu.make_async_copy(squares, squares, norm_recv).wait()
@@ -453,16 +451,14 @@
             pair((2, replicas)),
             pltpu.SemaphoreType.REGULAR,
             pltpu.VMEM((half - 1, over_rows, col_count), jnp.bfloat16),
-            pltpu.VMEM((half - 1, 1, LANES), jnp.int32),
+            pltpu.VMEM((replicas - 1, 1, LANES), jnp.int32),
             pltpu.VMEM((half - 1, slot_rows, col_count), jnp.bfloat16),
-            pltpu.VMEM((half, 1, LANES), jnp.int32),
             pltpu.VMEM((half, cap_rows, col_count), jnp.bfloat16),
             pltpu.VMEM((over_rows, col_count), jnp.bfloat16),
             pltpu.VMEM((over_rows, col_count), jnp.bfloat16),
             pair((2, half - 1)),
+            pair((2, 1)),
             pair((2, half - 1)),
-            pair((2, half - 1)),
-            pair((2, half)),
             pair((2, half)),
             pair((2, 1)),
             pltpu.VMEM((half // 2 - 1, over_rows, col_count), jnp.bfloat16),

time: 22 us -> 21.7 us (0.986)
  Pallas kernels: 20.6 us -> 20.3 us
    pallas_call x1, Pallas kernels: 16.9 us -> 16.4 us  [per_device(): pl.pallas_call(functools.partial(exchange, sections, replicas), out_shape...]
    pallas_call x1, Pallas kernels: 2.87 us -> 3.12 us  [per_device(): pl.pallas_call(functools.partial(residual_early, starts_early), out_shape...]
where the time goes in v6:
time: 21.7 us; the launch traced here: 21.6 us
  Pallas kernels  20.3 us (94%)
  between operations  1.29 us (6%)
    pallas_call x1, Pallas kernels, per_device(): pl.pallas_call(functools.partial(exchange, sections, replicas), out_shape...  16.4 us
    pallas_call x1, Pallas kernels, per_device(): pl.pallas_call(functools.partial(residual_early, starts_early), out_shape...  3.12 us
    pallas_call x1, Pallas kernels, per_device(): pl.pallas_call(functools.partial(deliver, replicas, starts_early), out_sh...  0.74 us

profile of v6, /device:TPU:0, one launch (start us, length us, event | category | flops | bytes accessed | tf_op | source)
XLA Modules:
  0.0 21.6 jit_solution(10372870939504632988)
XLA Ops:
  1.3 3.1 %shard_map.59.early_hbm = f32[16,8,4096]{2,1,0:T(8,128)} custom-call(s32[1,8]{1,0:T(1,128)} %ids_hbm.3, s32[1,1]{1,0:T(1,128)S(6)} %copy.8.counts_hbm, bf16[16,8,4096]{2,1,0:T(8,128)(2,1)} %bitcast.6, f32[16,8,4096]{2,1,0:T(8,128)} %bitcast.4), custom_call_target="tpu_custom_call" | custom-call | tf_op jit(solution)/shard_map/pallas_call | solution.py:420
  4.4 16.4 %shard_map.60 = (bf16[128,512]{1,0:T(8,128)(2,1)S(1)}, f32[8,16,8,512]{3,2,1,0:T(8,128)S(1)}) custom-call(s32[1,8]{1,0:T(1,128)} %ids_hbm.3, s32[1,1]{1,0:T(1,128)S(6)} %copy.8.counts_hbm, bf16[16,8,4096]{2,1,0:T(8,128)(2,1)} %bitcast.7, f32[16,8,4096]{2,1,0:T(8,128)} %bitcast.5, f32[16,8,4096]{2,1,0:T(8,128)} %shard_map.59.early_hbm), custom_call_target="tpu_custom_call" | custom-call | tf_op jit(solution)/shard_map/pallas_call | solution.py:435
  20.8 0.7 %shard_map.61 = (bf16[128,512]{1,0:T(8,128)(2,1)}, f32[16,8,4096]{2,1,0:T(8,128)}) custom-call(bf16[128,512]{1,0:T(8,128)(2,1)S(1)} %get-tuple-element.6.update_ref, f32[8,16,8,512]{3,2,1,0:T(8,128)S(1)} %get-tuple-element.7.left_ref, f32[16,8,4096]{2,1,0:T(8,128)} %shard_map.59.early_hbm), custom_call_target="tpu_custom_call", output_to_operand_aliasing={{1}: (2, {})} | custom-call | tf_op jit(solution)/shard_map/pallas_call | solution.py:482

commit v7 on v6

--- a/solution.py
+++ b/solution.py
@@ -226,7 +226,7 @@
         relay_in[mask].start()
     for mask in urgent:
         pack_slots(mask, 0, cap)
-    pl.when(inner)(functools.partial(start_far, beside))
+    pl.when(inner)(functools.partial(start_far, beside[::-1]))
     pack(half)
     pl.when(part_at == 2)(functools.partial(start_far, beyond[::-1]))
     for mask in order[half:]:
@@ -237,7 +237,7 @@
     @pl.when(part_at == 3)
     def _():
         start_far(beyond[::-1])
-        start_far(beside)
+        start_far(beside[::-1])
 
     @pl.when(part_at == 1)
     def _():
@@ -250,7 +250,7 @@
     @pl.when(part_at == 0)
     def _():
         pl.semaphore_wait(ready, 1)
-        start_far(beside)
+        start_far(beside[::-1])
         start_far(beyond[::-1])
 
     start_near(next_to[::-1] + same)

time: 21.7 us -> 21.7 us (level)
  no operation moved by 1% of the time
where the time goes in v7:
time: 21.7 us; the launch traced here: 21.6 us
  Pallas kernels  20.3 us (94%)
  between operations  1.29 us (6%)
    pallas_call x1, Pallas kernels, per_device(): pl.pallas_call(functools.partial(exchange, sections, replicas), out_shape...  16.4 us
    pallas_call x1, Pallas kernels, per_device(): pl.pallas_call(functools.partial(residual_early, starts_early), out_shape...  3.12 us
    pallas_call x1, Pallas kernels, per_device(): pl.pallas_call(functools.partial(deliver, replicas, starts_early), out_sh...  0.74 us

profile of v7, /device:TPU:0, one launch (start us, length us, event | category | flops | bytes accessed | tf_op | source)
XLA Modules:
  0.0 21.6 jit_solution(9382066362551218582)
XLA Ops:
  1.3 3.1 %shard_map.59.early_hbm = f32[16,8,4096]{2,1,0:T(8,128)} custom-call(s32[1,8]{1,0:T(1,128)} %ids_hbm.3, s32[1,1]{1,0:T(1,128)S(6)} %copy.8.counts_hbm, bf16[16,8,4096]{2,1,0:T(8,128)(2,1)} %bitcast.6, f32[16,8,4096]{2,1,0:T(8,128)} %bitcast.4), custom_call_target="tpu_custom_call" | custom-call | tf_op jit(solution)/shard_map/pallas_call | solution.py:420
  4.4 16.4 %shard_map.60 = (bf16[128,512]{1,0:T(8,128)(2,1)S(1)}, f32[8,16,8,512]{3,2,1,0:T(8,128)S(1)}) custom-call(s32[1,8]{1,0:T(1,128)} %ids_hbm.3, s32[1,1]{1,0:T(1,128)S(6)} %copy.8.counts_hbm, bf16[16,8,4096]{2,1,0:T(8,128)(2,1)} %bitcast.7, f32[16,8,4096]{2,1,0:T(8,128)} %bitcast.5, f32[16,8,4096]{2,1,0:T(8,128)} %shard_map.59.early_hbm), custom_call_target="tpu_custom_call" | custom-call | tf_op jit(solution)/shard_map/pallas_call | solution.py:435
  20.8 0.7 %shard_map.61 = (bf16[128,512]{1,0:T(8,128)(2,1)}, f32[16,8,4096]{2,1,0:T(8,128)}) custom-call(bf16[128,512]{1,0:T(8,128)(2,1)S(1)} %get-tuple-element.6.update_ref, f32[8,16,8,512]{3,2,1,0:T(8,128)S(1)} %get-tuple-element.7.left_ref, f32[16,8,4096]{2,1,0:T(8,128)} %shard_map.59.early_hbm), custom_call_target="tpu_custom_call", output_to_operand_aliasing={{1}: (2, {})} | custom-call | tf_op jit(solution)/shard_map/pallas_call | solution.py:482
